TPU v7x, 32 devices: a whole 2x2x4 slice. The times are simulated.
32 devices in a mesh: groups: 2 (over y), band: 4 (over z), chan: 4 (over x, core).
Axes of the slice: x: 2, y: 2, z: 4, core: 2. Of those that a mesh axis runs over, the one named last changes fastest.
Arguments:
- slide_region: float32 [16, 32, 8192], P('chan', ('groups', 'band')), parts along dimension 1, may hold values from -6 to 6
- row_taps: float32 [16, 257], P('chan'), may hold values from -0.375 to 0.375
- column_taps: float32 [16, 257], replicated, may hold values from -0.375 to 0.375
- channel_mix: float32 [16, 16], replicated, may hold values from -1.5 to 1.5
Outputs:
- filtered: float32 [16, 32, 8192], P('chan', ('groups', 'band')), parts along dimension 1
There are 2 independent parts, one for each index of `groups`. A program takes and returns all parts, laid end to end along the dimension named above; an argument that names none is the same for every part. Nothing has to cross between parts.
All inputs are finite; a program needn't handle non-finite values.
Results may differ from a plain program's by a relative error of at most 0.00007.
Values sent between devices are 32-bit elements; how exact they have to be, the bound alone decides.
A program may use at most 64 MiB of HBM per device.

v0:
```python
import jax
import jax.numpy as jnp
from jax import lax
from jax.sharding import PartitionSpec as P

precise = lax.Precision.HIGHEST


def band_tables(filter_taps, tile_size):
    channels, length = filter_taps.shape
    margin = (length - 1) // 2
    period = 4 * tile_size
    border = 3 * tile_size + length
    widened = jnp.pad(filter_taps, ((0, 0), (border, border)))
    lowest = margin - tile_size + border
    window = widened[:, lowest : lowest + 3 * tile_size]
    vector = jnp.pad(window, ((0, 0), (0, tile_size)))
    repeated = jnp.tile(vector, (1, tile_size))[:, : tile_size * (period - 1)]
    toeplitz = repeated.reshape(channels, tile_size, period - 1)[:, :, : 3 * tile_size]
    stacked = jnp.transpose(toeplitz, (0, 2, 1))
    return stacked.reshape(channels, 3, tile_size, tile_size)


def along_columns(signal, filter_taps):
    tile_size = 128
    tables = band_tables(filter_taps, tile_size)
    channels, row_count, col_count = signal.shape
    tile_count = col_count // tile_size
    tiled = signal.reshape(channels, row_count, tile_count, tile_size)
    padded = jnp.pad(tiled, ((0, 0), (0, 0), (1, 1), (0, 0)))
    result = jnp.einsum(
        "crti,cij->crtj", padded[:, :, 0:tile_count], tables[:, 0], precision=precise
    )
    result = result + jnp.einsum(
        "crti,cij->crtj", padded[:, :, 1 : tile_count + 1], tables[:, 1], precision=precise
    )
    result = result + jnp.einsum(
        "crti,cij->crtj", padded[:, :, 2:], tables[:, 2], precision=precise
    )
    return result.reshape(channels, row_count, col_count)


def along_rows(signal, filter_taps):
    channels, row_count, col_count = signal.shape
    tile_size = 128 if row_count % 128 == 0 else row_count
    tables = band_tables(filter_taps, tile_size)
    tile_count = row_count // tile_size
    tiled = signal.reshape(channels, tile_count, tile_size, col_count)
    padded = jnp.pad(tiled, ((0, 0), (1, 1), (0, 0), (0, 0)))
    result = jnp.einsum("ctiw,cij->ctjw", padded[:, 0:tile_count], tables[:, 0], precision=precise)
    result = result + jnp.einsum(
        "ctiw,cij->ctjw", padded[:, 1 : tile_count + 1], tables[:, 1], precision=precise
    )
    result = result + jnp.einsum("ctiw,cij->ctjw", padded[:, 2:], tables[:, 2], precision=precise)
    return result.reshape(channels, row_count, col_count)


def on_device(slide_region, row_taps, column_taps, channel_mix):
    local_channels = slide_region.shape[0]
    across = along_columns(slide_region, row_taps)
    column_band = lax.all_to_all(across, "band", split_axis=2, concat_axis=1, tiled=True)
    first_channel = lax.axis_index("chan") * local_channels
    own_taps = lax.dynamic_slice_in_dim(column_taps, first_channel, local_channels, 0)
    vertical = along_rows(column_band, own_taps)
    own_mixing = lax.dynamic_slice_in_dim(channel_mix, first_channel, local_channels, 0)
    blended = jnp.einsum(
        "oc,chw->ohw",
        own_mixing,
        lax.all_gather(vertical, "chan", axis=0, tiled=True),
        precision=precise,
    )
    return lax.all_to_all(blended, "band", split_axis=1, concat_axis=2, tiled=True)


def solution(mesh):
    in_specs = (P("chan", ("groups", "band"), None), P("chan", None), P(), P())
    out_specs = P("chan", ("groups", "band"), None)
    return jax.shard_map(
        on_device, mesh=mesh, in_specs=in_specs, out_specs=out_specs, check_vma=False
    )
```

profile of v0, /device:TPU:0, one launch (start us, length us, event | category | flops | bytes accessed | tf_op | source)
XLA Modules:
  0.0 165.2 jit_solution(12233661536541176305)
XLA Ops:
  6.5 0.0 copy-start
  6.5 0.7 pad_slice_fusion.4
  7.3 0.1 broadcast_bitcast_fusion
  7.4 0.7 copy.47
  8.1 0.1 slice.68
  8.1 0.0 copy-start.1
  8.2 1.0 reshape.47
  9.2 0.1 slice_bitcast_fusion
  9.2 0.3 copy.24
  9.5 0.0 copy-done.1
  9.5 0.4 reshape.46
  9.9 0.6 fusion.4
  10.5 0.6 fusion.5
  11.2 0.6 fusion.3
  11.8 8.6 %copy.38 = f32[4,4,64,128]{1,0,3,2:T(4,128)} copy(f32[4,4,64,128]{3,2,1,0:T(8,128)S(1)} %fusion.3) | data formatting | bytes 1048576 | tf_op jit(solution)/shard_map/reshape | solution.py:40
  20.4 24.6 %reshape.55 = f32[4,1,32768]{2,1,0:T(1,128)} reshape(f32[8192,4,4]{2,1,0:T(4,128)} %bitcast.68) | data formatting | bytes 1048576
  45.0 6.3 %all-to-all-start = ((f32[4,1,32768]{2,1,0:T(1,128)}), f32[4,1,32768]{2,1,0:T(1,128)S(1)}, u32[]{:S(2)}, u32[]{:S(2)}) async-start(f32[4,1,32768]{2,1,0:T(1,128)} %reshape.55), calls=%async_computation | async-start | bytes 1048576 | tf_op jit(solution)/shard_map/all_to_all | solution.py:61
  51.3 0.0 all-gather.2.cloned.1.call-start
  51.3 0.8 dynamic-slice
  52.1 0.1 tile.9
  52.2 0.1 reshape.44
  52.3 0.1 reshape.45
  52.4 0.1 fusion.17
  52.5 0.4 fusion.8
  52.9 13.0 %all-to-all-done = f32[4,1,32768]{2,1,0:T(1,128)S(1)} async-done(((f32[4,1,32768]{2,1,0:T(1,128)}), f32[4,1,32768]{2,1,0:T(1,128)S(1)}, u32[]{:S(2)}, u32[]{:S(2)}) %all-to-all-start) | async-done | bytes 524320 | tf_op jit(solution)/shard_map/all_to_all | solution.py:61
  65.8 0.5 broadcast.18
  66.3 2.2 %reduce = f32[4,32768]{1,0:T(4,128)S(1)} reduce(f32[4,1,32768]{2,1,0:T(1,128)S(1)} %all-to-all-done, f32[]{:T(128)} %broadcast.18), dimensions={1}, to_apply=%all_to_all.24.reduce_sub_computation | reduce | bytes 1048580 | tf_op jit(solution)/shard_map/all_to_all | solution.py:61
  68.5 28.0 %reshape.56 = f32[8192,4,4]{2,1,0:T(4,128)} reshape(f32[4,32768]{1,0:T(4,128)S(1)} %reduce) | data formatting | bytes 1048576
  96.5 13.4 %copy.30 = f32[4,4,4,2048]{3,0,2,1:T(4,128)S(1)} copy(f32[4,4,4,2048]{2,0,3,1:T(4,128)} %bitcast.69) | data formatting | bytes 1048576 | tf_op jit(solution)/shard_map/all_to_all | solution.py:61
  109.9 0.9 convolution_add_fusion.1
  110.8 1.1 convolution_add_fusion
  111.9 0.0 all-gather.2.cloned.1.call-update
  111.9 21.8 %all-gather.2.cloned.1.call-done = f32[16,16,2048]{2,1,0:T(8,128)} async-done(((f32[4,16,2048]{2,1,0:T(8,128)}), f32[16,16,2048]{2,1,0:T(8,128)}) %all-gather.2.cloned.1.call-update) | async-done | bytes 2097168 | tf_op jit(solution)/shard_map/all_gather | solution.py:69
  133.8 0.0 copy-done
  133.8 3.8 %fusion = f32[4,16,2048]{2,0,1:T(4,128)S(1)} fusion(f32[16,16,2048]{2,1,0:T(8,128)} %all-gather.2.cloned.1.call-done, f32[16,16]{1,0:T(8,128)S(1)} %copy-done, s32[]{:T(128)S(6)} %select_n.4), kind=kOutput, calls=%fused_computation.2 | convolution fusion | flops 25165824 | bytes 2623492 | tf_op jit(solution)/shard_map/oc,chw->ohw/dot_general | solution.py:66
  137.5 19.3 %all_to_all.33 = f32[4,16,2048]{2,0,1:T(4,128)S(1)} all-to-all(f32[4,16,2048]{2,0,1:T(4,128)S(1)} %fusion), channel_id=1, replica_groups=mesh['groups'=2,'band'=4,'chan'=4] {'band'}, dimensions={1} | all-to-all | bytes 1048576 | tf_op jit(solution)/shard_map/all_to_all | solution.py:72
  156.8 0.3 copy.34
  157.2 1.2 all_to_all.30
  (4 shorter events, 0.0 us)
Async XLA Ops:
  6.5 127.2 %copy-start = (f32[16,16]{1,0:T(8,128)S(1)}, f32[16,16]{1,0:T(8,128)}, u32[]{:S(2)}) copy-start(f32[16,16]{1,0:T(8,128)} %param.7) | copy-start | bytes 3076
  8.1 1.4 copy-start.1
  45.0 20.8 %all-to-all-start = ((f32[4,1,32768]{2,1,0:T(1,128)}), f32[4,1,32768]{2,1,0:T(1,128)S(1)}, u32[]{:S(2)}, u32[]{:S(2)}) async-start(f32[4,1,32768]{2,1,0:T(1,128)} %reshape.55), calls=%async_computation | async-start | bytes 1048576 | tf_op jit(solution)/shard_map/all_to_all | solution.py:61
  51.3 82.4 %all-gather.2.cloned.1.call-start = ((), (), s32[]{:S(2)}) async-start(), calls=%async_computation.2 | async-start | bytes 2621440 | tf_op jit(solution)/shard_map/all_gather | solution.py:69
Sparse Core Ops, SparseCore 0:
  112.1 21.6 all-gather.1
where the time goes:
time: 166 us; the launch traced here: 165 us
  local copies, waits for them, and re-layouts  81.1 us (49%)
  waiting for transfers between devices  34.8 us (21%)
  blocking collectives  19.3 us (12%)
  between operations  13.5 us (8%)
  matrix products  7.99 us (5%)
  starting transfers between devices  6.35 us (4%)
  other arithmetic  2.17 us (1%)
    unnamed x8, local copies, waits for them, and re-layouts  53.4 us
    all_gather x1, waiting for transfers between devices, on_device(): lax.all_gather(vertical, 'chan', axis=0, tiled=True)  21.8 us
    all_to_all x1, blocking collectives, on_device(): lax.all_to_all(blended, 'band', split_axis=1, concat_axis=2, tiled=True)  19.3 us
    all_to_all x2, local copies, waits for them, and re-layouts, on_device(): lax.all_to_all(across, 'band', split_axis=2, concat_axis=1, tiled=True)  13.9 us
    all_to_all x1, waiting for transfers between devices, on_device(): lax.all_to_all(across, 'band', split_axis=2, concat_axis=1, tiled=True)  13 us
    reshape x1, local copies, waits for them, and re-layouts, along_columns(): return result.reshape(channels, row_count, col_count)  8.62 us
    all_to_all x1, starting transfers between devices, on_device(): lax.all_to_all(across, 'band', split_axis=2, concat_axis=1, tiled=True)  6.35 us
    dot_general x1, matrix products, on_device(): jnp.einsum('oc,chw->ohw', own_mixing, lax.all_gather(vertical, 'chan', ax...  3.77 us
  transfers between devices with their start and end apart: 2, of which 2 were waited for; matrix products, arithmetic and copies ran while one was open for 1% of the time, Pallas kernels for 0%

commit v1 on v0

--- a/solution.py
+++ b/solution.py
@@ -58,7 +58,10 @@
 def on_device(slide_region, row_taps, column_taps, channel_mix):
     local_channels = slide_region.shape[0]
     across = along_columns(slide_region, row_taps)
-    column_band = lax.all_to_all(across, "band", split_axis=2, concat_axis=1, tiled=True)
+    column_band = jnp.concatenate(
+        lax.all_to_all(jnp.stack(jnp.split(across, lax.axis_size("band"), axis=2)), "band", 0, 0),
+        axis=1,
+    )
     first_channel = lax.axis_index("chan") * local_channels
     own_taps = lax.dynamic_slice_in_dim(column_taps, first_channel, local_channels, 0)
     vertical = along_rows(column_band, own_taps)

time: 166 us -> 89.8 us (0.54)
  local copies, waits for them, and re-layouts: 81.1 us -> 6.58 us
    unnamed x8 -> x6, local copies, waits for them, and re-layouts: 53.4 us -> 0.81 us
    all_to_all x2 -> x0, local copies, waits for them, and re-layouts: 13.9 us -> none  [on_device(): lax.all_to_all(across, 'band', split_axis=2, concat_axis=1, tiled=True)]
    reshape x1, local copies, waits for them, and re-layouts: 8.62 us -> 0.2 us  [along_columns(): return result.reshape(channels, row_count, col_count)]
    all_to_all x1 -> x0, other arithmetic: 2.17 us -> none  [on_device(): lax.all_to_all(across, 'band', split_axis=2, concat_axis=1, tiled=True)]
  transfers between devices with their start and end apart: 2 -> 2, of which waited for: 2 -> 2; matrix products, arithmetic and copies ran while one was open for 1% -> 2% of each run, Pallas kernels for 0% -> 0%
where the time goes in v1:
time: 89.8 us; the launch traced here: 89.5 us
  waiting for transfers between devices  34.8 us (39%)
  blocking collectives  19.3 us (21%)
  between operations  13.6 us (15%)
  matrix products  7.98 us (9%)
  local copies, waits for them, and re-layouts  6.58 us (7%)
  starting transfers between devices  6.35 us (7%)
  other arithmetic  0.92 us (1%)
    all_gather x1, waiting for transfers between devices, on_device(): lax.all_gather(vertical, 'chan', axis=0, tiled=True)  21.8 us
    all_to_all x1, blocking collectives, on_device(): lax.all_to_all(blended, 'band', split_axis=1, concat_axis=2, tiled=True)  19.3 us
    all_to_all x1, waiting for transfers between devices, on_device(): lax.all_to_all(jnp.stack(jnp.split(across, lax.axis_size('band'), axis=2)...  13 us
    all_to_all x1, starting transfers between devices, on_device(): lax.all_to_all(jnp.stack(jnp.split(across, lax.axis_size('band'), axis=2)...  6.35 us
    dot_general x1, matrix products, on_device(): jnp.einsum('oc,chw->ohw', own_mixing, lax.all_gather(vertical, 'chan', ax...  3.77 us
  transfers between devices with their start and end apart: 2, of which 2 were waited for; matrix products, arithmetic and copies ran while one was open for 2% of the time, Pallas kernels for 0%

profile of v1, /device:TPU:0, one launch (start us, length us, event | category | flops | bytes accessed | tf_op | source)
XLA Modules:
  0.0 89.5 jit_solution(15135651072376944974)
XLA Ops:
  6.5 0.0 copy-start
  6.5 0.7 pad_slice_fusion.4
  7.3 0.1 broadcast_bitcast_fusion
  7.4 0.7 copy.42
  8.1 0.1 slice.68
  8.1 0.0 copy-start.1
  8.2 1.0 %reshape.48 = f32[4,128,511]{2,1,0:T(8,128)S(1)} reshape(f32[4,65408]{1,0:T(4,128)S(1)} %slice.68) | data formatting | bytes 2093056 | tf_op jit(solution)/shard_map/reshape | solution.py:19
  9.2 0.1 slice_bitcast_fusion
  9.2 0.3 copy.17
  9.5 0.0 copy-done.1
  9.5 0.4 reshape.47
  9.9 0.6 fusion.4
  10.5 0.6 fusion.5
  11.2 0.6 fusion.3
  11.8 0.2 reshape.50
  12.0 0.2 copy_bitcast_fusion.2
  12.2 0.2 copy_bitcast_fusion
  12.4 0.9 %pad_maximum_fusion = f32[4,4,4,2048]{3,1,2,0:T(4,128)} fusion(f32[1,4,4,2048]{3,1,2,0:T(4,128)S(1)} %get-tuple-element.12, f32[1,4,4,2048]{3,1,2,0:T(4,128)S(1)} %get-tuple-element.13, f32[1,4,4,2048]{3,1,2,0:T(4,128)S(1)} %get-tuple-element.14, f32[1,4,4,2048]{3,1,2,0:T(4,128)S(1)} %get-tuple-element.15), kind=kLoop, calls=%fused_computation.12 | loop fusion | flops 393216 | bytes 1048576 | tf_op jit(solution)/shard_map/stack | solution.py:62
  13.3 6.3 %all-to-all-start = ((f32[4,4,4,2048]{3,1,2,0:T(4,128)}), f32[4,4,4,2048]{3,1,2,0:T(4,128)S(1)}, u32[]{:S(2)}, u32[]{:S(2)}) async-start(f32[4,4,4,2048]{3,1,2,0:T(4,128)} %pad_maximum_fusion), calls=%async_computation | async-start | bytes 1048576 | tf_op jit(solution)/shard_map/all_to_all | solution.py:62
  19.7 0.0 all-gather.2.cloned.1.call-start
  19.7 0.8 dynamic-slice
  20.4 0.1 tile.9
  20.5 0.1 reshape.45
  20.6 0.1 reshape.46
  20.7 0.1 fusion.18
  20.8 0.4 fusion.8
  21.2 13.0 %all-to-all-done = f32[4,4,4,2048]{3,1,2,0:T(4,128)S(1)} async-done(((f32[4,4,4,2048]{3,1,2,0:T(4,128)}), f32[4,4,4,2048]{3,1,2,0:T(4,128)S(1)}, u32[]{:S(2)}, u32[]{:S(2)}) %all-to-all-start) | async-done | bytes 524320 | tf_op jit(solution)/shard_map/all_to_all | solution.py:62
  34.1 0.8 convolution_add_fusion.1
  35.0 1.1 %convolution_add_fusion = f32[4,16,2048]{2,1,0:T(8,128)} fusion(f32[4,16,2048]{2,1,0:T(8,128)S(1)} %convolution_add_fusion.1, f32[4,16,16]{1,2,0:T(8,128)S(1)} %bitcast.79), kind=kOutput, calls=%fused_computation | convolution fusion | flops 25296896 | bytes 1052672 | tf_op jit(solution)/shard_map/ctiw,cij->ctjw/dot_general | solution.py:54
  36.1 0.0 all-gather.2.cloned.1.call-update
  36.2 21.8 %all-gather.2.cloned.1.call-done = f32[16,16,2048]{2,1,0:T(8,128)} async-done(((f32[4,16,2048]{2,1,0:T(8,128)}), f32[16,16,2048]{2,1,0:T(8,128)}) %all-gather.2.cloned.1.call-update) | async-done | bytes 2097168 | tf_op jit(solution)/shard_map/all_gather | solution.py:72
  58.0 0.0 copy-done
  58.0 3.8 %fusion = f32[4,16,2048]{2,0,1:T(4,128)S(1)} fusion(f32[16,16,2048]{2,1,0:T(8,128)} %all-gather.2.cloned.1.call-done, f32[16,16]{1,0:T(8,128)S(1)} %copy-done, s32[]{:T(128)S(6)} %select_n.4), kind=kOutput, calls=%fused_computation.2 | convolution fusion | flops 25165824 | bytes 2623492 | tf_op jit(solution)/shard_map/oc,chw->ohw/dot_general | solution.py:69
  61.8 19.3 %all_to_all.23 = f32[4,16,2048]{2,0,1:T(4,128)S(1)} all-to-all(f32[4,16,2048]{2,0,1:T(4,128)S(1)} %fusion), channel_id=1, replica_groups=mesh['groups'=2,'band'=4,'chan'=4] {'band'}, dimensions={1} | all-to-all | bytes 1048576 | tf_op jit(solution)/shard_map/all_to_all | solution.py:75
  81.0 0.3 copy.28
  81.4 1.2 %all_to_all.20 = f32[4,4,8192]{2,1,0:T(4,128)} reshape(f32[4,4,4,2048]{3,2,1,0:T(4,128)S(1)} %copy.28) | data formatting | bytes 1048576 | tf_op jit(solution)/shard_map/all_to_all | solution.py:75
  (5 shorter events, 0.1 us)
Async XLA Ops:
  6.5 51.5 %copy-start = (f32[16,16]{1,0:T(8,128)S(1)}, f32[16,16]{1,0:T(8,128)}, u32[]{:S(2)}) copy-start(f32[16,16]{1,0:T(8,128)} %param.7) | copy-start | bytes 3076
  8.1 1.4 %copy-start.1 = (f32[4,4,8192]{2,1,0:T(4,128)S(1)}, f32[4,4,8192]{2,1,0:T(4,128)}, u32[]{:S(2)}) copy-start(f32[4,4,8192]{2,1,0:T(4,128)} %param.4) | copy-start | bytes 1572868
  13.3 20.8 %all-to-all-start = ((f32[4,4,4,2048]{3,1,2,0:T(4,128)}), f32[4,4,4,2048]{3,1,2,0:T(4,128)S(1)}, u32[]{:S(2)}, u32[]{:S(2)}) async-start(f32[4,4,4,2048]{3,1,2,0:T(4,128)} %pad_maximum_fusion), calls=%async_computation | async-start | bytes 1048576 | tf_op jit(solution)/shard_map/all_to_all | solution.py:62
  19.7 38.3 %all-gather.2.cloned.1.call-start = ((), (), s32[]{:S(2)}) async-start(), calls=%async_computation.2 | async-start | bytes 2621440 | tf_op jit(solution)/shard_map/all_gather | solution.py:72
Sparse Core Ops, SparseCore 0:
  36.3 21.6 all-gather.1

commit v2 on v0

--- a/solution.py
+++ b/solution.py
@@ -4,6 +4,22 @@
 from jax.sharding import PartitionSpec as P
 
 precise = lax.Precision.HIGHEST
+
+
+def product_in_turn(x, axis, dim, product):
+    count, index, rows = (lax.axis_size(axis), lax.axis_index(axis), x.shape[dim])
+    right = [(i, (i + 1) % count) for i in range(count)]
+    behind = [(i, (i - 1) % count) for i in range(count)]
+    half = count // 2
+    from_left = from_right = x
+    total = product(x, index * rows)
+    for step in range(1, half + 1):
+        from_left = lax.ppermute(from_left, axis, right)
+        if step < count - half:
+            from_right = lax.ppermute(from_right, axis, behind)
+            total = total + product(from_right, (index + step) % count * rows)
+        total = total + product(from_left, (index - step) % count * rows)
+    return total
 
 
 def band_tables(filter_taps, tile_size):
@@ -63,11 +79,16 @@
     own_taps = lax.dynamic_slice_in_dim(column_taps, first_channel, local_channels, 0)
     vertical = along_rows(column_band, own_taps)
     own_mixing = lax.dynamic_slice_in_dim(channel_mix, first_channel, local_channels, 0)
-    blended = jnp.einsum(
-        "oc,chw->ohw",
-        own_mixing,
-        lax.all_gather(vertical, "chan", axis=0, tiled=True),
-        precision=precise,
+    blended = product_in_turn(
+        vertical,
+        "chan",
+        0,
+        lambda shard, offset: jnp.einsum(
+            "oc,chw->ohw",
+            lax.dynamic_slice_in_dim(own_mixing, offset, shard.shape[0], axis=1),
+            shard,
+            precision=precise,
+        ),
     )
     return lax.all_to_all(blended, "band", split_axis=1, concat_axis=2, tiled=True)
 

time: 166 us -> 147 us (0.89)
  between operations: 13.5 us -> 0.18 us
  waiting for transfers between devices: 34.8 us -> 28.2 us
  blocking collectives: 19.3 us -> 17.4 us
  starting transfers between devices: 6.35 us -> 8.24 us
    all_gather x1 -> x0, waiting for transfers between devices: 21.8 us -> none  [on_device(): lax.all_gather(vertical, 'chan', axis=0, tiled=True)]
    ppermute x0 -> x3, waiting for transfers between devices: none -> 15.3 us  [the longest x2 14.6 us: product_in_turn(): from_left = lax.ppermute(from_left, axis, right)]
    ppermute x0 -> x3, starting transfers between devices: none -> 1.89 us  [the longest x1 1.73 us: product_in_turn(): from_right = lax.ppermute(from_right, axis, behind)]
    all_to_all x1, blocking collectives: 19.3 us -> 17.4 us  [on_device(): lax.all_to_all(blended, 'band', split_axis=1, concat_axis=2, tiled=True)]
    dot_general x1 -> x4, matrix products: 3.77 us -> 5.18 us  [on_device(): jnp.einsum('oc,chw->ohw', lax.dynamic_slice_in_dim(own_mixing, offset, sh...]
    unnamed x8 -> x6, local copies, waits for them, and re-layouts: 53.4 us -> 53.4 us
  transfers between devices with their start and end apart: 2 -> 4, of which waited for: 2 -> 4; matrix products, arithmetic and copies ran while one was open for 1% -> 4% of each run, Pallas kernels for 0% -> 0%
where the time goes in v2:
time: 147 us
  local copies, waits for them, and re-layouts  82.3 us (56%)
  waiting for transfers between devices  28.2 us (19%)
  blocking collectives  17.4 us (12%)
  matrix products  8.33 us (6%)
  starting transfers between devices  8.24 us (6%)
  other arithmetic  2.17 us (1%)
    unnamed x6, local copies, waits for them, and re-layouts  53.4 us
    all_to_all x1, blocking collectives, on_device(): lax.all_to_all(blended, 'band', split_axis=1, concat_axis=2, tiled=True)  17.4 us
    ppermute x2, waiting for transfers between devices, product_in_turn(): from_left = lax.ppermute(from_left, axis, right)  14.6 us
    all_to_all x2, local copies, waits for them, and re-layouts, on_device(): lax.all_to_all(across, 'band', split_axis=2, concat_axis=1, tiled=True)  13.9 us
    all_to_all x1, waiting for transfers between devices, on_device(): lax.all_to_all(across, 'band', split_axis=2, concat_axis=1, tiled=True)  12.9 us
    reshape x1, local copies, waits for them, and re-layouts, along_columns(): return result.reshape(channels, row_count, col_count)  8.59 us
    all_to_all x1, starting transfers between devices, on_device(): lax.all_to_all(across, 'band', split_axis=2, concat_axis=1, tiled=True)  6.35 us
    dot_general x4, matrix products, on_device(): jnp.einsum('oc,chw->ohw', lax.dynamic_slice_in_dim(own_mixing, offset, sh...  5.18 us
  transfers between devices with their start and end apart: 4, of which 4 were waited for; matrix products, arithmetic and copies ran while one was open for 4% of the time, Pallas kernels for 0%

profile of v2, /device:TPU:0, one launch (start us, length us, event | category | flops | bytes accessed | tf_op | source)
XLA Modules:
  0.0 146.9 jit_solution(13429245418236757437)
XLA Ops:
  0.0 0.0 copy-start
  0.0 1.4 reshape.46
  1.4 0.7 pad_slice_fusion.4
  2.1 0.1 broadcast_bitcast_fusion
  2.3 0.7 copy.48
  2.9 0.1 slice.68
  3.0 1.0 reshape.47
  4.0 0.1 slice_bitcast_fusion
  4.1 0.3 copy.26
  4.4 0.6 fusion.3
  5.0 0.6 fusion.2
  5.6 0.6 fusion.1
  6.3 8.6 %copy.41 = f32[4,4,64,128]{1,0,3,2:T(4,128)} copy(f32[4,4,64,128]{3,2,1,0:T(8,128)S(1)} %fusion.1) | data formatting | bytes 1048576 | tf_op jit(solution)/shard_map/reshape | solution.py:56
  14.8 24.6 %reshape.58 = f32[4,1,32768]{2,1,0:T(1,128)} reshape(f32[8192,4,4]{2,1,0:T(4,128)} %bitcast.75) | data formatting | bytes 1048576
  39.4 6.4 %all-to-all-start = ((f32[4,1,32768]{2,1,0:T(1,128)}), f32[4,1,32768]{2,1,0:T(1,128)S(1)}, u32[]{:S(2)}, u32[]{:S(2)}) async-start(f32[4,1,32768]{2,1,0:T(1,128)} %reshape.58), calls=%async_computation | async-start | bytes 1048576 | tf_op jit(solution)/shard_map/all_to_all | solution.py:77
  45.8 0.8 dynamic-slice
  46.6 0.1 tile.9
  46.7 0.1 reshape.44
  46.8 0.1 reshape.45
  46.9 0.1 fusion.24
  47.0 0.4 fusion.10
  47.3 12.9 %all-to-all-done = f32[4,1,32768]{2,1,0:T(1,128)S(1)} async-done(((f32[4,1,32768]{2,1,0:T(1,128)}), f32[4,1,32768]{2,1,0:T(1,128)S(1)}, u32[]{:S(2)}, u32[]{:S(2)}) %all-to-all-start) | async-done | bytes 524320 | tf_op jit(solution)/shard_map/all_to_all | solution.py:77
  60.3 0.5 broadcast.21
  60.8 2.2 %reduce = f32[4,32768]{1,0:T(4,128)S(1)} reduce(f32[4,1,32768]{2,1,0:T(1,128)S(1)} %all-to-all-done, f32[]{:T(128)} %broadcast.21), dimensions={1}, to_apply=%all_to_all.24.reduce_sub_computation | reduce | bytes 1048580 | tf_op jit(solution)/shard_map/all_to_all | solution.py:77
  63.0 28.0 %reshape.59 = f32[8192,4,4]{2,1,0:T(4,128)} reshape(f32[4,32768]{1,0:T(4,128)S(1)} %reduce) | data formatting | bytes 1048576
  91.0 13.4 %copy.31 = f32[4,4,4,2048]{3,1,2,0:T(4,128)S(1)} copy(f32[4,4,4,2048]{1,0,3,2:T(4,128)} %bitcast.76) | data formatting | bytes 1048576 | tf_op jit(solution)/shard_map/all_to_all | solution.py:77
  104.4 0.2 reshape.50
  104.6 0.6 convolution_add_fusion.4
  105.1 0.4 convolution_add_fusion.3
  105.5 0.1 collective-permute-start.1
  105.6 1.7 %collective-permute-start = (f32[4,16,2048]{2,1,0:T(8,128)S(1)}, f32[4,16,2048]{2,1,0:T(8,128)S(1)}, u32[]{:S(2)}, u32[]{:S(2)}) collective-permute-start(f32[4,16,2048]{2,1,0:T(8,128)S(1)} %convolution_add_fusion.3), channel_id=1, source_target_pairs={{0,3},{1,0},{2,1},{3,2},{4,7},{5,4},{6,5},{7,6},{8,11},{9,8},{10,9... | collective-permute-start | bytes 1572872 | tf_op jit(solution)/shard_map/ppermute | solution.py:19
  107.3 0.0 copy-done
  107.3 1.3 fusion.7
  108.6 9.4 %collective-permute-done.1 = f32[4,16,2048]{2,1,0:T(8,128)S(1)} collective-permute-done((f32[4,16,2048]{2,1,0:T(8,128)S(1)}, f32[4,16,2048]{2,1,0:T(8,128)S(1)}, u32[]{:S(2)}, u32[]{:S(2)}) %collective-permute-start.1) | collective-permute-done | bytes 524320 | tf_op jit(solution)/shard_map/ppermute | solution.py:17
  118.0 0.1 collective-permute-start.2
  118.1 0.7 collective-permute-done
  118.8 1.3 convolution_add_fusion.2
  120.1 1.3 convolution_add_fusion.1
  121.4 5.2 %collective-permute-done.2 = f32[4,16,2048]{2,1,0:T(8,128)S(1)} collective-permute-done((f32[4,16,2048]{2,1,0:T(8,128)S(1)}, f32[4,16,2048]{2,1,0:T(8,128)S(1)}, u32[]{:S(2)}, u32[]{:S(2)}) %collective-permute-start.2) | collective-permute-done | bytes 524320 | tf_op jit(solution)/shard_map/ppermute | solution.py:17
  126.6 1.3 convolution_add_fusion
  127.9 17.4 %all_to_all.33 = f32[4,16,2048]{2,0,1:T(4,128)S(1)} all-to-all(f32[4,16,2048]{2,0,1:T(4,128)S(1)} %convolution_add_fusion), channel_id=1, replica_groups=mesh['groups'=2,'band'=4,'chan'=4] {'band'}, dimensions={1} | all-to-all | bytes 1048576 | tf_op jit(solution)/shard_map/all_to_all | solution.py:93
  145.3 0.3 copy.37
  145.7 1.2 all_to_all.30
  (4 shorter events, 0.0 us)
Async XLA Ops:
  0.0 107.3 %copy-start = (f32[16,16]{1,0:T(8,128)S(1)}, f32[16,16]{1,0:T(8,128)}, u32[]{:S(2)}) copy-start(f32[16,16]{1,0:T(8,128)} %param.7) | copy-start | bytes 3076
  39.4 20.8 %all-to-all-start = ((f32[4,1,32768]{2,1,0:T(1,128)}), f32[4,1,32768]{2,1,0:T(1,128)S(1)}, u32[]{:S(2)}, u32[]{:S(2)}) async-start(f32[4,1,32768]{2,1,0:T(1,128)} %reshape.58), calls=%async_computation | async-start | bytes 1048576 | tf_op jit(solution)/shard_map/all_to_all | solution.py:77
  105.5 12.5 %collective-permute-start.1 = (f32[4,16,2048]{2,1,0:T(8,128)S(1)}, f32[4,16,2048]{2,1,0:T(8,128)S(1)}, u32[]{:S(2)}, u32[]{:S(2)}) collective-permute-start(f32[4,16,2048]{2,1,0:T(8,128)S(1)} %convolution_add_fusion.3), channel_id=1, source_target_pairs={{0,1},{1,2},{2,3},{3,0},{4,5},{5,6},{6,7},{7,4},{8,9},{9,10},{10,1... | collective-permute-start | bytes 1572872 | tf_op jit(solution)/shard_map/ppermute | solution.py:17
  105.6 13.2 %collective-permute-start = (f32[4,16,2048]{2,1,0:T(8,128)S(1)}, f32[4,16,2048]{2,1,0:T(8,128)S(1)}, u32[]{:S(2)}, u32[]{:S(2)}) collective-permute-start(f32[4,16,2048]{2,1,0:T(8,128)S(1)} %convolution_add_fusion.3), channel_id=1, source_target_pairs={{0,3},{1,0},{2,1},{3,2},{4,7},{5,4},{6,5},{7,6},{8,11},{9,8},{10,9... | collective-permute-start | bytes 1572872 | tf_op jit(solution)/shard_map/ppermute | solution.py:19
  118.0 8.6 %collective-permute-start.2 = (f32[4,16,2048]{2,1,0:T(8,128)S(1)}, f32[4,16,2048]{2,1,0:T(8,128)S(1)}, u32[]{:S(2)}, u32[]{:S(2)}) collective-permute-start(f32[4,16,2048]{2,1,0:T(8,128)S(1)} %collective-permute-done.1), channel_id=1, source_target_pairs={{0,1},{1,2},{2,3},{3,0},{4,5},{5,6},{6,7},{7,4},{8,9},{9,10},{10,1... | collective-permute-start | bytes 1572872 | tf_op jit(solution)/shard_map/ppermute | solution.py:17
